TPU v7x, 32 devices: a whole 2x2x4 slice. The times are simulated.
32 devices in a mesh: dp: 8 (over z, x), expert: 4 (over y, core).
Axes of the slice: x: 2, y: 2, z: 4, core: 2. Of those that a mesh axis runs over, the one named last changes fastest.
Arguments:
- queries: bfloat16 [256, 2048], P(('dp', 'expert')), may hold values from -8 to 8
- fresh_key: bfloat16 [256, 256], P(('dp', 'expert')), may hold values from -4 to 4
- fresh_value: bfloat16 [256, 256], P(('dp', 'expert')), may hold values from -4 to 4
- cached_keys: bfloat16 [256, 128, 256], P(('dp', 'expert')), may hold values from -8 to 8
- cached_values: bfloat16 [256, 128, 256], P(('dp', 'expert')), may hold values from -4 to 4
- lengths: int32 [256], P(('dp', 'expert')), may hold values from 2 to 128
- sink_logit_rows: float32 [32], replicated, may hold values from 1 to 5
- residual: bfloat16 [256, 2880], P('dp', 'expert'), may hold values from -6 to 6
- o_weight: bfloat16 [2880, 2048], P('expert'), may hold values from -0.125 to 0.125
- norm_gain: float32 [2880], replicated, may hold values from 0.5 to 1.5
- expert_ids: int32 [256, 4], replicated, may hold values from 0 to 7, all different within a row; in each aligned block of 32 rows (0 to 31, 32 to 63, ...) at most 32 rows name the same one
- route_weights: float32 [256, 4], replicated, may hold values from 0.1 to 0.6
- w_gate_up: bfloat16 [8, 2, 2880, 2880], P('dp', None, 'expert'), may hold values from -0.109375 to 0.109375
- w_down: bfloat16 [8, 2880, 2880], P('dp', 'expert'), may hold values from -0.15625 to 0.15625
Outputs:
- layer_out: bfloat16 [256, 2880], P('dp', 'expert')
Inputs may be any that keep to these rules, and one draw needn't show every extreme that they name: `expert_ids`: each row names 4 different experts; among any aligned block of 32 rows no expert is named by more than 32 rows.
All inputs are finite; a program needn't handle non-finite values.
Results may differ from a plain program's by a relative error of at most 0.018.
Values may be sent and summed in bfloat16 or wider, within the bound.
No kernel may reach another device: no remote copies, remote signals or barrier semaphores. Data moves between devices by JAX's collectives and lax.ppermute only.
A program may use at most 64 MiB of HBM per device.

v0:
```python
import math
import jax
import jax.numpy as jnp
from jax import lax
from jax.sharding import PartitionSpec as P

D = 2880
QUERY_HEADS = 32
KEY_VALUE_HEADS = 4
HEAD_SIZE = 64
WINDOW_LENGTH = 128
TOP = 4
norm_eps = 1e-05
swish_alpha = 1.702


def attend(queries, fresh_key, fresh_value, cached_keys, cached_values, lengths, sink_logit_rows):
    batch_count = queries.shape[0]
    head_groups = QUERY_HEADS // KEY_VALUE_HEADS
    query_head_rows = queries.reshape(batch_count, KEY_VALUE_HEADS, head_groups, HEAD_SIZE)
    key_rows = cached_keys.reshape(batch_count, WINDOW_LENGTH, KEY_VALUE_HEADS, HEAD_SIZE)
    value_rows = cached_values.reshape(batch_count, WINDOW_LENGTH, KEY_VALUE_HEADS, HEAD_SIZE)
    score_scale = 1.0 / math.sqrt(HEAD_SIZE)
    cache_scores = (
        jnp.einsum("bkgd,bwkd->bkgw", query_head_rows, key_rows, preferred_element_type=jnp.float32)
        * score_scale
    )
    own_scores = (
        jnp.einsum(
            "npwm,npm->npw",
            query_head_rows,
            fresh_key.reshape(batch_count, KEY_VALUE_HEADS, HEAD_SIZE),
            preferred_element_type=jnp.float32,
        )
        * score_scale
    )
    slots = jnp.arange(WINDOW_LENGTH, dtype=jnp.int32)
    valid = (slots[None, :] >= (WINDOW_LENGTH - lengths)[:, None])[:, None, None, :]
    sink_terms = sink_logit_rows.reshape(KEY_VALUE_HEADS, head_groups)[None]
    masked = jnp.where(valid, cache_scores, -jnp.inf)
    top = jnp.maximum(jnp.maximum(jnp.max(masked, axis=-1), own_scores), sink_terms)
    cache_exp = jnp.where(valid, jnp.exp(masked - top[..., None]), 0.0)
    self_exp = jnp.exp(own_scores - top)
    total = jnp.sum(cache_exp, axis=-1) + self_exp + jnp.exp(sink_terms - top)
    cache_prob = (cache_exp / total[..., None]).astype(jnp.bfloat16)
    own_probability = (self_exp / total).astype(jnp.bfloat16)
    blended = jnp.einsum(
        "bkgw,bwkd->bkgd", cache_prob, value_rows, preferred_element_type=jnp.float32
    )
    blended = blended + own_probability.astype(jnp.float32)[..., None] * fresh_value.reshape(
        batch_count, KEY_VALUE_HEADS, 1, HEAD_SIZE
    ).astype(jnp.float32)
    return blended.reshape(batch_count, QUERY_HEADS * HEAD_SIZE).astype(jnp.bfloat16)


def slot_onehot(named, capacity):
    counts = jnp.cumsum(named.astype(jnp.int32), axis=1) - 1
    places = jnp.arange(capacity, dtype=jnp.int32)
    return named[:, None, :] & (counts[:, None, :] == places[None, :, None])


def receiver_slots(expert_ids, route_weights, expert, blocks, capacity):
    picked = expert_ids == expert
    named = jnp.any(picked, axis=1).reshape(blocks, -1)
    weight_at = jnp.sum(jnp.where(picked, route_weights, 0.0), axis=1).reshape(blocks, -1)
    onehot = slot_onehot(named, capacity)
    slot_weight = jnp.sum(jnp.where(onehot, weight_at[:, None, :], 0.0), axis=2)
    return (onehot, slot_weight)


def sender_slots(my_ids, experts, capacity):
    labels = jnp.arange(experts, dtype=jnp.int32)
    named = jnp.any(my_ids[None, :, :] == labels[:, None, None], axis=2)
    return slot_onehot(named, capacity)


def body(
    queries,
    fresh_key,
    fresh_value,
    cached_keys,
    cached_values,
    lengths,
    sink_logit_rows,
    residual,
    o_weight,
    norm_gain,
    expert_ids,
    route_weights,
    w_gate_up,
    w_down,
):
    attended = attend(
        queries, fresh_key, fresh_value, cached_keys, cached_values, lengths, sink_logit_rows
    )
    projected = lax.dot_general(
        lax.all_gather(attended, "expert", axis=0, tiled=True),
        o_weight,
        (((1,), (1,)), ((), ())),
        preferred_element_type=jnp.float32,
    )
    stream = (residual.astype(jnp.float32) + projected).astype(jnp.bfloat16)
    wide = stream.astype(jnp.float32)
    group_rows = stream.shape[0]
    columns = stream.shape[1]
    experts = lax.axis_size("dp")
    capacity = 2 * group_rows * TOP // experts
    gain_cols = lax.dynamic_slice_in_dim(norm_gain, lax.axis_index("expert") * columns, columns)
    squares = lax.psum(jnp.sum(wide * wide, axis=1), "expert")
    score_scale = lax.rsqrt(squares / D + norm_eps)
    outgoing = (wide * score_scale[:, None] * gain_cols[None, :]).astype(jnp.bfloat16)
    onehot_in, slot_weight = receiver_slots(
        expert_ids, route_weights, lax.axis_index("dp"), experts, capacity
    )
    my_ids = lax.dynamic_slice_in_dim(expert_ids, lax.axis_index("dp") * group_rows, group_rows, 0)
    onehot_out = sender_slots(my_ids, experts, capacity)
    outbound = jnp.einsum(
        "ect,td->ecd", onehot_out.astype(jnp.bfloat16), outgoing, preferred_element_type=jnp.float32
    ).astype(jnp.bfloat16)
    received = lax.all_to_all(outbound, "dp", split_axis=0, concat_axis=0, tiled=True)
    rows = received.reshape(experts * capacity, columns)
    gate_up = w_gate_up[0]
    down = w_down[0]
    both = jnp.einsum(
        "rc,hfc->rhf",
        lax.all_gather(rows, "expert", axis=1, tiled=True),
        gate_up,
        preferred_element_type=jnp.float32,
    )
    gate = both[:, 0]
    up = both[:, 1]
    hidden = ((up + 1.0) * gate * jax.nn.sigmoid(swish_alpha * gate)).astype(jnp.bfloat16)
    summed = lax.psum_scatter(
        lax.dot_general(
            down, hidden, (((0,), (1,)), ((), ())), preferred_element_type=jnp.float32
        ).astype(jnp.bfloat16),
        "expert",
        scatter_dimension=0,
        tiled=True,
    ).astype(jnp.float32)
    contribution = (summed * slot_weight.reshape(1, -1)).astype(jnp.bfloat16)
    contribution = contribution.T.reshape(experts, capacity, columns)
    returned = lax.all_to_all(contribution, "dp", split_axis=0, concat_axis=0, tiled=True)
    returned_sum = jnp.einsum(
        "ect,ecd->td",
        onehot_out.astype(jnp.float32),
        returned.astype(jnp.float32),
        precision=lax.Precision.HIGHEST,
    )
    return (wide + returned_sum).astype(jnp.bfloat16)


def solution(mesh):
    placed = (
        P(("dp", "expert"), None),
        P(("dp", "expert"), None),
        P(("dp", "expert"), None),
        P(("dp", "expert"), None, None),
        P(("dp", "expert"), None, None),
        P(("dp", "expert")),
        P(),
        P("dp", "expert"),
        P("expert", None),
        P(),
        P(),
        P(),
        P("dp", None, "expert", None),
        P("dp", "expert", None),
    )
    return jax.shard_map(
        body, mesh=mesh, in_specs=placed, out_specs=P("dp", "expert"), check_vma=False
    )
```

profile of v0, /device:TPU:0, one launch (start us, length us, event | category | flops | bytes accessed | tf_op | source)
XLA Modules:
  0.0 138.2 jit_solution(12964307490870638373)
XLA Ops:
  6.5 0.0 copy-start
  6.5 0.0 copy-start.4
  6.5 0.0 all-gather.2.cloned.1.call-start
  6.5 0.8 broadcast_subtract_fusion
  7.4 0.1 iota_compare_fusion.3
  7.4 0.0 copy-start.3
  7.4 0.9 reshape.81
  8.4 1.3 copy.27
  9.7 1.4 reshape.94
  11.1 0.7 max.14
  11.8 0.9 fusion.48
  12.7 0.3 fusion.47
  13.0 0.0 copy-start.1
  13.0 0.2 fusion.28
  13.2 0.4 copy-done.1
  13.6 0.6 fusion.42
  14.3 1.3 copy.28
  15.6 0.0 copy-done.4
  15.6 0.7 reshape.87
  16.3 0.0 copy-done.3
  16.3 1.4 %fusion.12 = bf16[8,4,8,64]{3,2,1,0:T(8,128)(2,1)S(1)} fusion(bf16[8,128,4,64]{1,3,2,0:T(8,128)(2,1)S(1)} %bitcast.48, f32[8,4,8,128]{3,2,1,0:T(8,128)} %copy-done.1, f32[8,4,64]{2,1,0:T(4,128)} %reshape.87, f32[8,4,8]{2,1,0:T(4,128)} %get-tuple-element.7, f32[8,4,8]{2,1,0:T(4,128)} %get-tuple-element.8, f32[8,4,8]{2,1,0:T(4,128)S(1)} %maximum_maximum_fusion, ...), kind=kOutput, calls=%fused_computation.11 | convolution fusion | flops 4374528 | bytes 700416 | tf_op jit(solution)/shard_map/bkgw,bwkd->bkgd/dot_general | solution.py:47
  17.7 0.1 convert_element_type.86
  17.8 6.5 %all_gather.6 = bf16[32,2048]{1,0:T(8,128)(2,1)S(1)} all-gather(bf16[8,2048]{1,0:T(8,128)(2,1)S(1)} %convert_element_type.86), channel_id=1, replica_groups=mesh['dp'=8,'expert'=4] {'expert'}, dimensions={0}, use_global_device_ids=true | all-gather | bytes 163840 | tf_op jit(solution)/shard_map/all_gather | solution.py:97
  24.4 0.0 copy-done
  24.4 1.9 %multiply_reduce_fusion = (f32[32]{0:T(128)S(1)}, f32[32,720]{1,0:T(8,128)S(1)}) fusion(bf16[32,2048]{1,0:T(8,128)(2,1)S(1)} %all_gather.6, bf16[720,2048]{1,0:T(8,128)(2,1)S(1)} %copy-done, bf16[32,720]{1,0:T(8,128)(2,1)} %param.21), kind=kOutput, calls=%fused_computation.35 | convolution fusion | flops 94510048 | bytes 3218560 | tf_op jit(solution)/shard_map/dot_general | solution.py:96
  26.2 7.5 %psum.7 = f32[32]{0:T(128)S(1)} all-reduce(f32[32]{0:T(128)S(1)} %get-tuple-element.11), channel_id=1, replica_groups=mesh['dp'=8,'expert'=4] {'expert'}, use_global_device_ids=true, to_apply=%region_5.6 | all-reduce | flops 32 | bytes 256 | tf_op jit(solution)/shard_map/psum | solution.py:109
  33.7 0.8 constant_dynamic-slice_fusion
  34.5 0.2 reduce_window_sum.17
  34.7 0.8 dynamic_slice.7
  35.4 0.4 convolution_convert_fusion
  35.8 16.2 %all_to_all.10 = bf16[8,32,720]{2,1,0:T(8,128)(2,1)S(1)} all-to-all(bf16[8,32,720]{2,1,0:T(8,128)(2,1)S(1)} %convolution_convert_fusion), channel_id=1, replica_groups=mesh['dp'=8,'expert'=4] {'dp'}, dimensions={0} | all-to-all | bytes 737280 | tf_op jit(solution)/shard_map/all_to_all | solution.py:120
  52.1 0.9 copy.30
  53.0 0.0 all-gather.2.cloned.1.call-update
  53.0 0.0 reduce-scatter.2.cloned.1.call-start
  53.1 17.9 %all-gather.2.cloned.1.call-done = bf16[256,2880]{0,1:T(8,128)(2,1)} async-done(((bf16[256,720]{0,1:T(8,128)(2,1)}), bf16[256,2880]{0,1:T(8,128)(2,1)}) %all-gather.2.cloned.1.call-update) | async-done | bytes 1474576 | tf_op jit(solution)/shard_map/all_gather | solution.py:126
  71.0 6.3 %fusion = f32[256,2,720]{0,2,1:T(8,128)S(1)} fusion(bf16[1,2,720,2880]{3,2,1,0:T(8,128)(2,1)} %param.26, bf16[256,2880]{0,1:T(8,128)(2,1)} %all-gather.2.cloned.1.call-done), kind=kOutput, calls=%fused_computation | convolution fusion | flops 2123366400 | bytes 11243520 | tf_op jit(solution)/shard_map/rc,hfc->rhf/dot_general | solution.py:124
  77.3 0.0 copy-start.2
  77.3 0.0 copy-start.5
  77.3 5.3 %fusion.7 = bf16[2880,256]{1,0:T(8,128)(2,1)} fusion(bf16[1,720,2880]{2,1,0:T(8,128)(2,1)} %param.27, f32[256,2,720]{0,2,1:T(8,128)S(1)} %fusion), kind=kOutput, calls=%fused_computation.5 | convolution fusion | flops 1063895040 | bytes 7096320 | tf_op jit(solution)/shard_map/dot_general | solution.py:134
  82.6 0.0 reduce-scatter.2.cloned.1.call-update
  82.6 0.0 copy-done.2
  82.6 0.1 and.22
  82.7 0.2 reduce_window_sum.18
  82.9 0.0 copy-done.5
  83.0 0.1 broadcast_in_dim.55
  83.0 0.1 select_reduce_fusion
  83.2 0.1 mul.93
  83.2 27.0 %reduce-scatter.2.cloned.1.call-done = bf16[720,256]{1,0:T(8,128)(2,1)} async-done(((bf16[2880,256]{1,0:T(8,128)(2,1)}), bf16[720,256]{1,0:T(8,128)(2,1)}) %reduce-scatter.2.cloned.1.call-update) | async-done | bytes 368656 | tf_op jit(solution)/shard_map/reduce_scatter | solution.py:133
  110.2 1.8 %fusion.20 = bf16[256,720]{0,1:T(8,128)(2,1)} fusion(bf16[720,256]{1,0:T(8,128)(2,1)} %reduce-scatter.2.cloned.1.call-done, f32[256]{0:T(256)S(1)} %mul.93), kind=kLoop, calls=%fused_computation.23 | loop fusion | flops 552960 | bytes 738304 | tf_op jit(solution)/shard_map/transpose | solution.py:142
  112.0 1.2 copy.31
  113.2 17.2 %all_to_all.11 = bf16[8,32,720]{2,1,0:T(8,128)(2,1)S(1)} all-to-all(bf16[8,32,720]{2,1,0:T(8,128)(2,1)S(1)} %bitcast.47), channel_id=1, replica_groups=mesh['dp'=8,'expert'=4] {'dp'}, dimensions={0} | all-to-all | bytes 737280 | tf_op jit(solution)/shard_map/all_to_all | solution.py:143
  130.4 1.0 fusion.16
  (9 shorter events, 0.1 us)
Async XLA Ops:
  6.5 17.8 %copy-start = (bf16[720,2048]{1,0:T(8,128)(2,1)S(1)}, bf16[720,2048]{1,0:T(8,128)(2,1)}, u32[]{:S(2)}) copy-start(bf16[720,2048]{1,0:T(8,128)(2,1)} %param.22) | copy-start | bytes 8847364
  6.5 9.1 %copy-start.4 = (bf16[8,256]{1,0:T(8,128)(2,1)S(1)}, bf16[8,256]{1,0:T(8,128)(2,1)}, u32[]{:S(2)}) copy-start(bf16[8,256]{1,0:T(8,128)(2,1)} %param.16) | copy-start | bytes 12292
  6.5 64.4 %all-gather.2.cloned.1.call-start = ((), (), s32[]{:S(2)}) async-start(), calls=%async_computation.3 | async-start | bytes 1843200 | tf_op jit(solution)/shard_map/all_gather | solution.py:126
  7.4 8.9 %copy-start.3 = (pred[8,128]{1,0:T(8,128)(4,1)}, pred[8,128]{1,0:T(8,128)(4,1)S(1)}, u32[]{:S(2)}) copy-start(pred[8,128]{1,0:T(8,128)(4,1)S(1)} %iota_compare_fusion.3) | copy-start | bytes 3076
  13.0 0.6 copy-start.1
  53.0 57.2 %reduce-scatter.2.cloned.1.call-start = ((), (), s32[]{:S(2)}) async-start(), calls=%async_computation.4 | async-start | bytes 1843200 | tf_op jit(solution)/shard_map/reduce_scatter | solution.py:133
  77.3 5.3 %copy-start.2 = (s32[256,4]{0,1:T(4,128)S(1)}, s32[256,4]{0,1:T(4,128)}, u32[]{:S(2)}) copy-start(s32[256,4]{0,1:T(4,128)} %param.24) | copy-start | bytes 12292
  77.3 5.6 %copy-start.5 = (f32[256,4]{0,1:T(4,128)S(1)}, f32[256,4]{0,1:T(4,128)}, u32[]{:S(2)}) copy-start(f32[256,4]{0,1:T(4,128)} %param.25) | copy-start | bytes 12292
Sparse Core Ops, SparseCore 0:
  53.1 17.7 all-gather.1
  82.7 27.4 reduce-scatter.1
where the time goes:
time: 139 us; the launch traced here: 138 us
  blocking collectives  47.5 us (34%)
  waiting for transfers between devices  44.9 us (32%)
  matrix products  17.4 us (13%)
  between operations  13.5 us (10%)
  local copies, waits for them, and re-layouts  10.8 us (8%)
  other arithmetic  4.1 us (3%)
    reduce_scatter x1, waiting for transfers between devices, body(): lax.psum_scatter(lax.dot_general(down, hidden, (((0,), (1,)), ((), ())),...  27 us
    all_gather x1, waiting for transfers between devices, body(): lax.all_gather(rows, 'expert', axis=1, tiled=True)  17.9 us
    all_to_all x1, blocking collectives, body(): lax.all_to_all(contribution, 'dp', split_axis=0, concat_axis=0, tiled=True)  17.2 us
    all_to_all x1, blocking collectives, body(): lax.all_to_all(outbound, 'dp', split_axis=0, concat_axis=0, tiled=True)  16.2 us
    psum x1, blocking collectives, body(): squares = lax.psum(jnp.sum(wide * wide, axis=1), 'expert')  7.47 us
    all_gather x1, blocking collectives, body(): lax.all_gather(attended, 'expert', axis=0, tiled=True)  6.54 us
    dot_general x1, matrix products, body(): jnp.einsum('rc,hfc->rhf', lax.all_gather(rows, 'expert', axis=1, tiled=Tr...  6.32 us
    dot_general x1, matrix products, body(): lax.dot_general(down, hidden, (((0,), (1,)), ((), ())), preferred_element...  5.28 us
  transfers between devices with their start and end apart: 2, of which 2 were waited for; matrix products, arithmetic and copies ran while one was open for 0% of the time, Pallas kernels for 0%

commit v1 on v0

--- a/solution.py
+++ b/solution.py
@@ -121,12 +121,38 @@
     rows = received.reshape(experts * capacity, columns)
     gate_up = w_gate_up[0]
     down = w_down[0]
-    both = jnp.einsum(
+    size, here, rows_2 = (lax.axis_size("expert"), lax.axis_index("expert"), rows.shape[1])
+    forward = [(i, (i + 1) % size) for i in range(size)]
+    left = [(i, (i - 1) % size) for i in range(size)]
+    half = size // 2
+    from_left = from_right = rows
+    total_2 = jnp.einsum(
         "rc,hfc->rhf",
-        lax.all_gather(rows, "expert", axis=1, tiled=True),
-        gate_up,
+        rows,
+        lax.dynamic_slice_in_dim(gate_up, here * rows_2, rows.shape[1], axis=2),
         preferred_element_type=jnp.float32,
     )
+    for step in range(1, half + 1):
+        from_left = lax.ppermute(from_left, "expert", forward)
+        if step < size - half:
+            from_right = lax.ppermute(from_right, "expert", left)
+            total_2 = total_2 + jnp.einsum(
+                "rc,hfc->rhf",
+                from_right,
+                lax.dynamic_slice_in_dim(
+                    gate_up, (here + step) % size * rows_2, from_right.shape[1], axis=2
+                ),
+                preferred_element_type=jnp.float32,
+            )
+        total_2 = total_2 + jnp.einsum(
+            "rc,hfc->rhf",
+            from_left,
+            lax.dynamic_slice_in_dim(
+                gate_up, (here - step) % size * rows_2, from_left.shape[1], axis=2
+            ),
+            preferred_element_type=jnp.float32,
+        )
+    both = total_2
     gate = both[:, 0]
     up = both[:, 1]
     hidden = ((up + 1.0) * gate * jax.nn.sigmoid(swish_alpha * gate)).astype(jnp.bfloat16)

time: 139 us -> 130 us (0.935)
  waiting for transfers between devices: 44.9 us -> 32.6 us
  matrix products: 17.4 us -> 20.4 us
  starting transfers between devices: 0.04 us -> 2.05 us
    all_gather x1 -> x0, waiting for transfers between devices: 17.9 us -> none  [body(): lax.all_gather(rows, 'expert', axis=1, tiled=True)]
    ppermute x0 -> x3, waiting for transfers between devices: none -> 5.87 us  [the longest x2 5.86 us: body(): from_left = lax.ppermute(from_left, 'expert', forward)]
    dot_general x1 -> x4, matrix products: 6.32 us -> 11.4 us  [the longest x2 5.71 us: body(): jnp.einsum('rc,hfc->rhf', from_left, lax.dynamic_slice_in_dim(gate_up, (h...]
    dot_general x1, matrix products: 5.28 us -> 3.16 us  [body(): lax.dot_general(down, hidden, (((0,), (1,)), ((), ())), preferred_element...]
    ppermute x0 -> x3, starting transfers between devices: none -> 2.05 us  [the longest x1 1.74 us: body(): from_right = lax.ppermute(from_right, 'expert', left)]
    unnamed x14 -> x16, local copies, waits for them, and re-layouts: 3.05 us -> 3.54 us
  transfers between devices with their start and end apart: 2 -> 4, of which waited for: 2 -> 3; matrix products, arithmetic and copies ran while one was open for 0% -> 7% of each run, Pallas kernels for 0% -> 0%
where the time goes in v1:
time: 130 us; the launch traced here: 129 us
  blocking collectives  47.5 us (37%)
  waiting for transfers between devices  32.6 us (25%)
  matrix products  20.4 us (16%)
  between operations  13.6 us (10%)
  local copies, waits for them, and re-layouts  9.86 us (8%)
  other arithmetic  3.35 us (3%)
  starting transfers between devices  2.05 us (2%)
    reduce_scatter x1, waiting for transfers between devices, body(): lax.psum_scatter(lax.dot_general(down, hidden, (((0,), (1,)), ((), ())),...  26.7 us
    all_to_all x1, blocking collectives, body(): lax.all_to_all(contribution, 'dp', split_axis=0, concat_axis=0, tiled=True)  17.3 us
    all_to_all x1, blocking collectives, body(): lax.all_to_all(outbound, 'dp', split_axis=0, concat_axis=0, tiled=True)  16.2 us
    psum x1, blocking collectives, body(): squares = lax.psum(jnp.sum(wide * wide, axis=1), 'expert')  7.48 us
    all_gather x1, blocking collectives, body(): lax.all_gather(attended, 'expert', axis=0, tiled=True)  6.54 us
    ppermute x2, waiting for transfers between devices, body(): from_left = lax.ppermute(from_left, 'expert', forward)  5.86 us
    dot_general x2, matrix products, body(): jnp.einsum('rc,hfc->rhf', from_left, lax.dynamic_slice_in_dim(gate_up, (h...  5.71 us
    unnamed x16, local copies, waits for them, and re-layouts  3.54 us
  transfers between devices with their start and end apart: 4, of which 3 were waited for; matrix products, arithmetic and copies ran while one was open for 7% of the time, Pallas kernels for 0%

profile of v1, /device:TPU:0, one launch (start us, length us, event | category | flops | bytes accessed | tf_op | source)
XLA Modules:
  0.0 129.3 jit_solution(2684317064069445579)
XLA Ops:
  6.5 0.0 copy-start
  6.5 0.0 copy-start.2
  6.5 0.0 copy-start.4
  6.5 0.0 reduce-scatter.2.cloned.1.call-start
  6.6 2.2 %copy.32 = bf16[8,128,256]{1,2,0:T(8,128)(2,1)} copy(bf16[8,128,256]{2,1,0:T(8,128)(2,1)} %param.18) | data formatting | bytes 1048576 | tf_op args[4]
  8.7 0.0 copy-start.1
  8.7 0.9 reshape.85
  9.6 1.3 %copy.31 = bf16[8,128,256]{1,2,0:T(8,128)(2,1)S(1)} copy(bf16[8,128,256]{2,1,0:T(8,128)(2,1)} %param.17) | data formatting | bytes 1048576 | tf_op args[3]
  11.0 0.7 broadcast_subtract_fusion
  11.6 0.1 iota_compare_fusion.3
  11.7 1.4 %reshape.91 = f32[8,4,64]{2,1,0:T(4,128)} reshape(bf16[8,256]{1,0:T(8,128)(2,1)} %param.16) | data formatting | bytes 12288 | tf_op jit(solution)/shard_map/convert_element_type | solution.py:52
  13.1 0.0 copy-done.2
  13.1 0.7 reshape.101
  13.8 0.0 copy-done.4
  13.8 0.1 max.14
  13.8 0.9 fusion.66
  14.7 0.3 fusion.65
  15.1 0.2 fusion.42
  15.3 1.5 %fusion.23 = bf16[8,4,8,64]{3,2,1,0:T(8,128)(2,1)S(1)} fusion(bf16[8,128,4,64]{1,3,2,0:T(8,128)(2,1)} %bitcast.69, f32[8,4,8,128]{3,2,1,0:T(8,128)S(1)} %get-tuple-element.10, f32[8,4,64]{2,1,0:T(4,128)} %reshape.91, f32[8,4,8]{2,1,0:T(4,128)S(1)} %get-tuple-element.7, f32[8,4,8]{2,1,0:T(4,128)S(1)} %get-tuple-element.8, ...), kind=kOutput, calls=%fused_computation.21 | convolution fusion | flops 4374528 | bytes 700416 | tf_op jit(solution)/shard_map/bkgw,bwkd->bkgd/dot_general | solution.py:47
  16.8 0.1 convert_element_type.86
  17.0 6.5 %all_gather.3 = bf16[32,2048]{1,0:T(8,128)(2,1)S(1)} all-gather(bf16[8,2048]{1,0:T(8,128)(2,1)S(1)} %convert_element_type.86), channel_id=1, replica_groups=mesh['dp'=8,'expert'=4] {'expert'}, dimensions={0}, use_global_device_ids=true | all-gather | bytes 163840 | tf_op jit(solution)/shard_map/all_gather | solution.py:97
  23.5 0.0 copy-done.1
  23.5 0.1 constant_dynamic-slice_fusion
  23.6 0.2 reduce_window_sum.17
  23.8 0.0 copy-done
  23.8 1.9 %multiply_reduce_fusion = (f32[32]{0:T(128)S(1)}, f32[32,720]{1,0:T(8,128)S(1)}) fusion(bf16[32,2048]{1,0:T(8,128)(2,1)S(1)} %all_gather.3, bf16[720,2048]{1,0:T(8,128)(2,1)S(1)} %copy-done, bf16[32,720]{1,0:T(8,128)(2,1)} %param.21), kind=kOutput, calls=%fused_computation.48 | convolution fusion | flops 94510048 | bytes 3218560 | tf_op jit(solution)/shard_map/dot_general | solution.py:96
  25.6 7.5 %psum.7 = f32[32]{0:T(128)S(1)} all-reduce(f32[32]{0:T(128)S(1)} %get-tuple-element.11), channel_id=1, replica_groups=mesh['dp'=8,'expert'=4] {'expert'}, use_global_device_ids=true, to_apply=%region_5.6 | all-reduce | flops 32 | bytes 256 | tf_op jit(solution)/shard_map/psum | solution.py:109
  33.1 0.8 dynamic_slice.27
  33.9 0.4 convolution_convert_fusion
  34.3 16.2 %all_to_all.10 = bf16[8,32,720]{2,1,0:T(8,128)(2,1)S(1)} all-to-all(bf16[8,32,720]{2,1,0:T(8,128)(2,1)S(1)} %convolution_convert_fusion), channel_id=1, replica_groups=mesh['dp'=8,'expert'=4] {'dp'}, dimensions={0} | all-to-all | bytes 737280 | tf_op jit(solution)/shard_map/all_to_all | solution.py:120
  50.5 0.9 copy.35
  51.4 0.0 collective-permute-start.1
  51.4 1.7 %collective-permute-start = (bf16[256,720]{0,1:T(8,128)(2,1)}, bf16[256,720]{0,1:T(8,128)(2,1)S(1)}, u32[]{:S(2)}, u32[]{:S(2)}) collective-permute-start(bf16[256,720]{0,1:T(8,128)(2,1)} %copy.35), channel_id=1, source_target_pairs={{0,3},{1,0},{2,1},{3,2},{4,7},{5,4},{6,5},{7,6},{8,11},{9,8},{10,9... | collective-permute-start | bytes 1105928 | tf_op jit(solution)/shard_map/ppermute | solution.py:138
  53.2 2.7 %fusion.14 = f32[256,2,720]{0,2,1:T(8,128)S(1)} fusion(bf16[256,720,1]{1,0,2:T(8,128)(2,1)S(1)} %bitcast.66, bf16[1,2,720,2880]{3,2,1,0:T(8,128)(2,1)} %param.26, s32[]{:T(128)S(6)} %select_n.49), kind=kOutput, calls=%fused_computation.10 | convolution fusion | flops 530841600 | bytes 4055044 | tf_op jit(solution)/shard_map/rc,hfc->rhf/dot_general | solution.py:129
  55.9 4.9 %collective-permute-done.1 = bf16[256,720]{0,1:T(8,128)(2,1)} collective-permute-done((bf16[256,720]{0,1:T(8,128)(2,1)}, bf16[256,720]{0,1:T(8,128)(2,1)}, u32[]{:S(2)}, u32[]{:S(2)}) %collective-permute-start.1) | collective-permute-done | bytes 368672 | tf_op jit(solution)/shard_map/ppermute | solution.py:136
  60.8 0.3 collective-permute-start.2
  61.1 2.9 %fusion.10 = f32[256,2,720]{0,2,1:T(8,128)S(1)} fusion(bf16[1,2,720,2880]{3,2,1,0:T(8,128)(2,1)} %param.26, s32[]{:T(128)S(6)} %select_n.53, bf16[256,720]{0,1:T(8,128)(2,1)} %collective-permute-done.1), kind=kOutput, calls=%fused_computation.6 | convolution fusion | flops 530841600 | bytes 4055044 | tf_op jit(solution)/shard_map/rc,hfc->rhf/dot_general | solution.py:147
  64.0 0.0 collective-permute-done
  64.0 0.0 slice-start
  64.0 2.9 %fusion.12 = f32[256,2,720]{0,2,1:T(8,128)S(1)} fusion(bf16[1,2,720,2880]{3,2,1,0:T(8,128)(2,1)} %param.26, s32[]{:T(128)S(6)} %select_n.51, bf16[256,720]{0,1:T(8,128)(2,1)S(1)} %collective-permute-done), kind=kOutput, calls=%fused_computation.8 | convolution fusion | flops 530841600 | bytes 4055044 | tf_op jit(solution)/shard_map/rc,hfc->rhf/dot_general | solution.py:139
  66.9 0.0 slice-start.1
  66.9 1.0 collective-permute-done.2
  67.9 2.8 %add_add_fusion = f32[256,2,720]{0,2,1:T(8,128)S(1)} fusion(f32[256,2,720]{0,2,1:T(8,128)S(1)} %fusion.10, f32[256,2,720]{0,2,1:T(8,128)S(1)} %fusion.14, f32[256,2,720]{0,2,1:T(8,128)S(1)} %fusion.12, bf16[1,2,720,2880]{3,2,1,0:T(8,128)(2,1)} %param.26, s32[]{:T(128)S(6)} %select_n.55, bf16[256,720]{0,1:T(8,128)(2,1)S(1)} %collective-permute-done.2), kind=kOutput, calls=%fused_computation.16 | convolution fusion | flops 531947520 | bytes 8478724 | tf_op jit(solution)/shard_map/rc,hfc->rhf/dot_general | solution.py:147
  70.8 0.0 slice-done
  70.8 0.0 slice-done.1
  70.8 0.0 copy-start.3
  70.8 3.2 %fusion.5 = bf16[2880,256]{1,0:T(8,128)(2,1)} fusion(bf16[1,720,2880]{2,1,0:T(8,128)(2,1)S(1)} %bitcast.73, f32[256,2,720]{0,2,1:T(8,128)S(1)} %add_add_fusion), kind=kOutput, calls=%fused_computation.3 | convolution fusion | flops 1063895040 | bytes 7096320 | tf_op jit(solution)/shard_map/dot_general | solution.py:160
  74.0 0.0 reduce-scatter.2.cloned.1.call-update
  74.0 0.0 copy-done.3
  74.0 0.1 broadcast_in_dim.55
  74.1 0.1 and.38
  74.2 0.2 reduce_window_sum.18
  74.4 0.1 select_reduce_fusion
  74.5 0.1 mul.106
  74.6 26.7 %reduce-scatter.2.cloned.1.call-done = bf16[720,256]{1,0:T(8,128)(2,1)} async-done(((bf16[2880,256]{1,0:T(8,128)(2,1)}), bf16[720,256]{1,0:T(8,128)(2,1)}) %reduce-scatter.2.cloned.1.call-update) | async-done | bytes 368656 | tf_op jit(solution)/shard_map/reduce_scatter | solution.py:159
  101.3 1.8 %fusion.31 = bf16[256,720]{0,1:T(8,128)(2,1)} fusion(bf16[720,256]{1,0:T(8,128)(2,1)} %reduce-scatter.2.cloned.1.call-done, f32[256]{0:T(256)S(1)} %mul.106), kind=kLoop, calls=%fused_computation.33 | loop fusion | flops 552960 | bytes 738304 | tf_op jit(solution)/shard_map/transpose | solution.py:168
  103.1 1.2 copy.37
  104.3 17.3 %all_to_all.11 = bf16[8,32,720]{2,1,0:T(8,128)(2,1)S(1)} all-to-all(bf16[8,32,720]{2,1,0:T(8,128)(2,1)S(1)} %bitcast.68), channel_id=1, replica_groups=mesh['dp'=8,'expert'=4] {'dp'}, dimensions={0} | all-to-all | bytes 737280 | tf_op jit(solution)/shard_map/all_to_all | solution.py:169
  121.5 1.0 fusion.27
  (11 shorter events, 0.1 us)
Async XLA Ops:
  6.5 17.3 %copy-start = (bf16[720,2048]{1,0:T(8,128)(2,1)S(1)}, bf16[720,2048]{1,0:T(8,128)(2,1)}, u32[]{:S(2)}) copy-start(bf16[720,2048]{1,0:T(8,128)(2,1)} %param.22) | copy-start | bytes 8847364
  6.5 6.5 %copy-start.2 = (bf16[8,256]{1,0:T(8,128)(2,1)S(1)}, bf16[8,256]{1,0:T(8,128)(2,1)}, u32[]{:S(2)}) copy-start(bf16[8,256]{1,0:T(8,128)(2,1)} %param.15) | copy-start | bytes 12292
  6.5 7.2 %copy-start.4 = (f32[32]{0:T(128)S(1)}, f32[32]{0:T(128)}, u32[]{:S(2)}) copy-start(f32[32]{0:T(128)} %param.20) | copy-start | bytes 388
  6.5 94.8 %reduce-scatter.2.cloned.1.call-start = ((), (), s32[]{:S(2)}) async-start(), calls=%async_computation.3 | async-start | bytes 1843200 | tf_op jit(solution)/shard_map/reduce_scatter | solution.py:159
  8.7 14.8 %copy-start.1 = (s32[256,4]{0,1:T(4,128)S(1)}, s32[256,4]{0,1:T(4,128)}, u32[]{:S(2)}) copy-start(s32[256,4]{0,1:T(4,128)} %param.24) | copy-start | bytes 12292
  51.4 9.3 %collective-permute-start.1 = (bf16[256,720]{0,1:T(8,128)(2,1)}, bf16[256,720]{0,1:T(8,128)(2,1)}, u32[]{:S(2)}, u32[]{:S(2)}) collective-permute-start(bf16[256,720]{0,1:T(8,128)(2,1)} %copy.35), channel_id=1, source_target_pairs={{0,1},{1,2},{2,3},{3,0},{4,5},{5,6},{6,7},{7,4},{8,9},{9,10},{10,1... | collective-permute-start | bytes 1105928 | tf_op jit(solution)/shard_map/ppermute | solution.py:136
  51.4 12.5 %collective-permute-start = (bf16[256,720]{0,1:T(8,128)(2,1)}, bf16[256,720]{0,1:T(8,128)(2,1)S(1)}, u32[]{:S(2)}, u32[]{:S(2)}) collective-permute-start(bf16[256,720]{0,1:T(8,128)(2,1)} %copy.35), channel_id=1, source_target_pairs={{0,3},{1,0},{2,1},{3,2},{4,7},{5,4},{6,5},{7,6},{8,11},{9,8},{10,9... | collective-permute-start | bytes 1105928 | tf_op jit(solution)/shard_map/ppermute | solution.py:138
  60.8 7.1 %collective-permute-start.2 = (bf16[256,720]{0,1:T(8,128)(2,1)}, bf16[256,720]{0,1:T(8,128)(2,1)S(1)}, u32[]{:S(2)}, u32[]{:S(2)}) collective-permute-start(bf16[256,720]{0,1:T(8,128)(2,1)} %collective-permute-done.1), channel_id=1, source_target_pairs={{0,1},{1,2},{2,3},{3,0},{4,5},{5,6},{6,7},{7,4},{8,9},{9,10},{10,1... | collective-permute-start | bytes 1105928 | tf_op jit(solution)/shard_map/ppermute | solution.py:136
  64.0 6.8 %slice-start = ((s8[4239360]{0:T(1024)(128)(4,1)}), s8[4194304]{0:T(1024)(128)(4,1)S(1)}, s32[]{:S(2)}) async-start(s8[4239360]{0:T(1024)(128)(4,1)} %bitcast.72), calls=%async_computation.4 | async-start | bytes 8388608
  66.9 3.9 %slice-start.1 = ((s8[4239360]{0:T(1024)(128)(4,1)}), s8[45056]{0:T(1024)(128)(4,1)S(1)}, s32[]{:S(2)}) async-start(s8[4239360]{0:T(1024)(128)(4,1)} %bitcast.72), calls=%async_computation.5 | async-start | bytes 90112
  70.8 3.2 %copy-start.3 = (f32[256,4]{0,1:T(4,128)S(1)}, f32[256,4]{0,1:T(4,128)}, u32[]{:S(2)}) copy-start(f32[256,4]{0,1:T(4,128)} %param.25) | copy-start | bytes 12292
Sparse Core Ops, SparseCore 0:
  74.1 27.1 reduce-scatter.1
